TPU v7x, 32 devices: a whole 2x2x4 slice. The times are simulated.
32 devices in a mesh: groups: 2 (over y), seq: 4 (over z), head: 2 (over x), rep: 2 (over core).
Axes of the slice: x: 2, y: 2, z: 4, core: 2. Of those that a mesh axis runs over, the one named last changes fastest.
Arguments:
- queries: bfloat16 [128, 64, 128], P(('groups', 'seq', 'rep'), 'head'), parts along dimension 0, may hold values from -256 to 256
- page_owner: int32 [128, 128], P(('groups', 'seq', 'rep')), parts along dimension 0, may hold values from -1 to 3, as said below
- page_slot: int32 [128, 128], P(('groups', 'seq', 'rep')), parts along dimension 0, may hold values from -1 to 63, as said below
- lengths: int32 [128], P(('groups', 'seq', 'rep')), parts along dimension 0, may hold values from 1 to 16384, as said below
- keys: bfloat16 [1024, 8, 128, 128], P(('groups', 'seq', 'rep'), 'head'), parts along dimension 0, may hold values from -24 to 24
- values: bfloat16 [1024, 8, 128, 128], P(('groups', 'seq', 'rep'), 'head'), parts along dimension 0, may hold values from -6 to 6
Outputs:
- attended: bfloat16 [128, 64, 128], P(('groups', 'seq', 'rep'), 'head'), parts along dimension 0
There are 2 independent parts, one for each index of `groups`. A program takes and returns all parts, laid end to end along the dimension named above; each array names one. Nothing has to cross between parts.
Inputs may be any that keep to these rules, and one draw needn't show every extreme that they name: `page_owner`: for j below ceil(lengths[r] / 128) the seq index of the device, among those of r's half (r // 8) % 2, whose pool holds page j of r; -1 for later j. `page_slot`: the page's slot in that pool, -1 where page_owner is -1. No slot of a pool holds two pages; in each half, some device's pool has all 64 slots in use. `lengths`: in each half some request has the most.
All inputs are finite; a program needn't handle non-finite values.
Results may differ from a plain program's by a relative error of at most 0.0041.
Values may be sent and summed in bfloat16 or wider, within the bound.
A program may use at most 64 MiB of HBM per device.

v0:
```python
import math
import jax
import jax.numpy as jnp
from jax import lax
from jax.sharding import PartitionSpec as P

masked_score = -1e30


def on_device(queries, page_owner, page_slot, lengths, keys, values):
    rows_own = queries.shape[0]
    head_count = queries.shape[1]
    head_width = queries.shape[2]
    pool_size = keys.shape[0]
    kv_heads = keys.shape[1]
    page_tokens = keys.shape[2]
    group_size = head_count // kv_heads
    most_pages = page_owner.shape[1]
    page_index = jnp.arange(most_pages, dtype=jnp.int32)
    all_queries, all_owner, all_slot, all_length = (
        lax.all_gather(queries, "seq", axis=0, tiled=True),
        lax.all_gather(page_owner, "seq", axis=0, tiled=True),
        lax.all_gather(page_slot, "seq", axis=0, tiled=True),
        lax.all_gather(lengths, "seq", axis=0, tiled=True),
    )
    live_count = jnp.clip(all_length[:, None] - page_index[None, :] * page_tokens, 0, page_tokens)
    rows_half = all_queries.shape[0]
    seq_index = lax.axis_index("seq")
    held_here = (all_owner == seq_index) & (live_count > 0)
    slot_index = jnp.arange(pool_size, dtype=jnp.int32)
    matches = held_here[None, :, :] & (all_slot[None, :, :] == slot_index[:, None, None])
    slot_owner = jnp.any(matches, axis=2)
    slot_tokens = jnp.sum(jnp.where(matches, live_count[None, :, :], 0), axis=(1, 2))
    picker = slot_owner.astype(jnp.bfloat16)
    flat_queries = all_queries.reshape(rows_half, head_count * head_width)
    slot_queries = jnp.dot(picker, flat_queries, preferred_element_type=jnp.float32)
    slot_queries = slot_queries.astype(jnp.bfloat16).reshape(
        pool_size, kv_heads, group_size, head_width
    )
    score_scale = 1.0 / math.sqrt(head_width)
    scores = (
        jnp.einsum("pkgd,pktd->pkgt", slot_queries, keys, preferred_element_type=jnp.float32)
        * score_scale
    )
    token_index = jnp.arange(page_tokens, dtype=jnp.int32)
    live_tokens = (token_index[None, :] < slot_tokens[:, None])[:, None, None, :]
    scores = jnp.where(live_tokens, scores, masked_score)
    page_max = jnp.max(scores, axis=3)
    weights = jnp.where(live_tokens, jnp.exp(scores - page_max[..., None]), 0.0)
    page_sum = jnp.sum(weights, axis=3)
    page_out = jnp.einsum(
        "pkgt,pktd->pkgd", weights.astype(jnp.bfloat16), values, preferred_element_type=jnp.float32
    )
    linked = slot_owner.T[:, :, None, None]
    request_max = jnp.max(jnp.where(linked, page_max[None], masked_score), axis=1)
    rescale = jnp.where(
        linked, jnp.exp(jnp.minimum(page_max[None] - request_max[:, None], 0.0)), 0.0
    )
    request_sum = jnp.sum(rescale * page_sum[None], axis=1)
    request_out = jnp.einsum("rpkg,pkgd->rkgd", rescale, page_out, precision=lax.Precision.HIGHEST)
    got_max, got_sum, got_out = (
        lax.all_to_all(request_max, "seq", split_axis=0, concat_axis=0, tiled=True),
        lax.all_to_all(request_sum, "seq", split_axis=0, concat_axis=0, tiled=True),
        lax.all_to_all(request_out, "seq", split_axis=0, concat_axis=0, tiled=True),
    )
    sources = rows_half // rows_own
    got_max = got_max.reshape((sources, rows_own) + got_max.shape[1:])
    got_sum = got_sum.reshape((sources, rows_own) + got_sum.shape[1:])
    got_out = got_out.reshape((sources, rows_own) + got_out.shape[1:])
    overall = jnp.max(got_max, axis=0)
    source_scale = jnp.exp(got_max - overall[None])
    own_sum = jnp.sum(source_scale * got_sum, axis=0)
    own_out = jnp.sum(source_scale[..., None] * got_out, axis=0)
    attended = own_out / own_sum[..., None]
    return attended.astype(jnp.bfloat16).reshape(rows_own, head_count, head_width)


def solution(mesh):
    placed = (
        P(("groups", "seq", "rep"), "head", None),
        P(("groups", "seq", "rep"), None),
        P(("groups", "seq", "rep"), None),
        P(("groups", "seq", "rep")),
        P(("groups", "seq", "rep"), "head", None, None),
        P(("groups", "seq", "rep"), "head", None, None),
    )
    return jax.shard_map(
        on_device,
        mesh=mesh,
        in_specs=placed,
        out_specs=P(("groups", "seq", "rep"), "head", None),
        check_vma=False,
    )
```

profile of v0, /device:TPU:0, one launch (start us, length us, event | category | flops | bytes accessed | tf_op | source)
XLA Modules:
  0.0 100.2 jit_solution(10780645562737073349)
XLA Ops:
  0.0 1.2 %dynamic-slice = u32[1]{0:T(128)} dynamic-slice(u32[32]{0:T(128)} %constant.28, u32[]{:T(128)S(6)} %add), dynamic_slice_sizes={1} | dynamic-slice | bytes 12
  1.9 0.9 dynamic-update-slice
  2.8 9.9 %all-reduce = s32[32]{0:T(128)S(1)} all-reduce(s32[32]{0:T(128)S(1)} %dynamic-update-slice), channel_id=1, replica_groups=mesh['groups'=2,'seq'=4,'head'=2,'rep'=2] {'seq'}, use_global_device_ids=true, to_apply=%add | all-reduce | flops 32 | bytes 256
  12.7 13.3 %all_gather.12 = s32[32,128]{1,0:T(8,128)S(1)} all-gather(s32[8,128]{1,0:T(8,128)} %param.7), channel_id=1, replica_groups=mesh['groups'=2,'seq'=4,'head'=2,'rep'=2] {'seq'}, dimensions={0}, use_global_device_ids=true | all-gather | bytes 20480 | tf_op jit(solution)/shard_map/all_gather | solution.py:22
  26.0 13.3 %all_gather.14 = s32[32,128]{1,0:T(8,128)S(1)} all-gather(s32[8,128]{1,0:T(8,128)} %param.8), channel_id=1, replica_groups=mesh['groups'=2,'seq'=4,'head'=2,'rep'=2] {'seq'}, dimensions={0}, use_global_device_ids=true | all-gather | bytes 20480 | tf_op jit(solution)/shard_map/all_gather | solution.py:23
  39.5 1.2 %fusion.4 = pred[64,32]{1,0:T(8,128)(4,1)S(1)} fusion(s32[32,128]{1,0:T(8,128)S(1)} %all_gather.14, pred[32,128]{1,0:T(8,128)(4,1)S(1)} %compare_and_fusion), kind=kLoop, calls=%fused_computation.10 | loop fusion | flops 784384 | bytes 22528 | tf_op jit(solution)/shard_map/reduce_or | solution.py:32
  40.7 1.2 %select_reduce_fusion = s32[64]{0:T(128)S(1)} fusion(s32[32,128]{1,0:T(8,128)S(1)} %subtract_clamp_fusion, s32[32,128]{1,0:T(8,128)S(1)} %all_gather.14, pred[32,128]{1,0:T(8,128)(4,1)S(1)} %compare_and_fusion), kind=kLoop, calls=%fused_computation.7 | loop fusion | flops 1048512 | bytes 37120 | tf_op jit(solution)/shard_map/reduce_sum | solution.py:33
  42.0 14.0 %all_gather.15 = bf16[32,32,128]{2,1,0:T(8,128)(2,1)S(1)} all-gather(bf16[8,32,128]{2,1,0:T(8,128)(2,1)} %param.6), channel_id=1, replica_groups=mesh['groups'=2,'seq'=4,'head'=2,'rep'=2] {'seq'}, dimensions={0}, use_global_device_ids=true | all-gather | bytes 327680 | tf_op jit(solution)/shard_map/all_gather | solution.py:21
  56.0 0.3 fusion.1
  56.4 6.9 %fusion.22 = (f32[64,4,8]{2,1,0:T(4,128)S(1)}, f32[64,4,8,128]{3,2,1,0:T(8,128)S(1)}) fusion(bf16[64,4,8,128]{3,2,1,0:T(8,128)(2,1)S(1)} %bitcast.21, bf16[64,4,128,128]{3,2,1,0:T(8,128)(2,1)} %param.10, pred[64,128]{1,0:T(8,128)(4,1)S(1)} %iota_compare_fusion.1), kind=kOutput, calls=%fused_computation.38 | convolution fusion | flops 67893248 | bytes 9977856 | tf_op jit(solution)/shard_map/pkgd,pktd->pkgt/dot_general | solution.py:42
  63.4 0.8 fusion.5
  64.4 0.2 select_reduce_fusion.1
  64.6 0.4 multiply_reduce_fusion
  65.1 0.7 reshape.94
  65.8 3.2 %all-to-all-start.2 = ((f32[4,1,256]{2,1,0:T(1,128)}), f32[4,1,256]{2,1,0:T(1,128)S(1)}, u32[]{:S(2)}, u32[]{:S(2)}) async-start(f32[4,1,256]{2,1,0:T(1,128)} %reshape.94), calls=%async_computation.2 | async-start | bytes 8192 | tf_op jit(solution)/shard_map/all_to_all | solution.py:63
  69.1 4.7 %fusion.7 = f32[64,4,8,128]{3,2,1,0:T(8,128)S(1)} fusion(bf16[64,4,128,128]{3,2,1,0:T(8,128)(2,1)} %param.11, f32[64,4,8,128]{3,2,1,0:T(8,128)S(1)} %get-tuple-element.8, f32[64,4,8]{2,1,0:T(4,128)S(1)} %get-tuple-element.7, pred[64,128]{1,0:T(8,128)(4,1)S(1)} %iota_compare_fusion.1), kind=kOutput, calls=%fused_computation.13 | convolution fusion | flops 67895296 | bytes 10502144 | tf_op jit(solution)/shard_map/pkgt,pktd->pkgd/dot_general | solution.py:51
  73.9 0.7 reshape.92
  74.6 5.0 %all-to-all-start = ((f32[4,1,256]{2,1,0:T(1,128)}), f32[4,1,256]{2,1,0:T(1,128)S(1)}, u32[]{:S(2)}, u32[]{:S(2)}) async-start(f32[4,1,256]{2,1,0:T(1,128)} %reshape.92), calls=%async_computation | async-start | bytes 8192 | tf_op jit(solution)/shard_map/all_to_all | solution.py:62
  79.7 1.6 %convolution_bitcast_fusion = f32[32,4,8,128]{3,0,2,1:T(8,128)S(1)} fusion(f32[64,4,8,128]{3,2,1,0:T(8,128)S(1)} %fusion.7, f32[32,4,8]{0,2,1:T(8,128)S(1)} %select_reduce_fusion.1, f32[64,4,8]{0,2,1:T(8,128)S(1)} %copy.30, pred[32,64]{1,0:T(8,128)(4,1)S(1)} %copy.29), kind=kOutput, calls=%fused_computation.4 | convolution fusion | flops 100859904 | bytes 1587200 | tf_op jit(solution)/shard_map/rpkg,pkgd->rkgd/dot_general | solution.py:60
  81.3 1.1 %copy.35 = f32[32,4,8,128]{3,2,1,0:T(8,128)} copy(f32[32,4,8,128]{3,0,2,1:T(8,128)S(1)} %convolution_bitcast_fusion) | data formatting | bytes 1048576 | tf_op jit(solution)/shard_map/rpkg,pkgd->rkgd/transpose | solution.py:60
  82.4 2.9 %all-to-all-done = f32[4,1,256]{2,1,0:T(1,128)S(1)} async-done(((f32[4,1,256]{2,1,0:T(1,128)}), f32[4,1,256]{2,1,0:T(1,128)S(1)}, u32[]{:S(2)}, u32[]{:S(2)}) %all-to-all-start) | async-done | bytes 4128 | tf_op jit(solution)/shard_map/all_to_all | solution.py:62
  85.3 3.5 %all-to-all-start.1 = ((f32[32,4,8,128]{3,2,1,0:T(8,128)}), f32[32,4,8,128]{3,2,1,0:T(8,128)S(1)}, u32[]{:S(2)}, u32[]{:S(2)}) async-start(f32[32,4,8,128]{3,2,1,0:T(8,128)} %copy.35), calls=%async_computation.1 | async-start | bytes 1048576 | tf_op jit(solution)/shard_map/all_to_all | solution.py:64
  88.8 0.5 broadcast.55
  89.3 0.7 reduce
  90.0 0.1 reshape.95
  90.1 0.1 copy.39
  90.2 0.7 reduce.1
  90.9 0.1 reshape.93
  91.0 0.1 copy.33
  91.4 7.7 %all-to-all-done.1 = f32[32,4,8,128]{3,2,1,0:T(8,128)S(1)} async-done(((f32[32,4,8,128]{3,2,1,0:T(8,128)}), f32[32,4,8,128]{3,2,1,0:T(8,128)S(1)}, u32[]{:S(2)}, u32[]{:S(2)}) %all-to-all-start.1) | async-done | bytes 524320 | tf_op jit(solution)/shard_map/all_to_all | solution.py:64
  99.1 0.3 fusion.9
  99.4 0.7 fusion.19
  (16 shorter events, 1.0 us)
Async XLA Ops:
  65.8 8.8 %all-to-all-start.2 = ((f32[4,1,256]{2,1,0:T(1,128)}), f32[4,1,256]{2,1,0:T(1,128)S(1)}, u32[]{:S(2)}, u32[]{:S(2)}) async-start(f32[4,1,256]{2,1,0:T(1,128)} %reshape.94), calls=%async_computation.2 | async-start | bytes 8192 | tf_op jit(solution)/shard_map/all_to_all | solution.py:63
  74.6 10.7 %all-to-all-start = ((f32[4,1,256]{2,1,0:T(1,128)}), f32[4,1,256]{2,1,0:T(1,128)S(1)}, u32[]{:S(2)}, u32[]{:S(2)}) async-start(f32[4,1,256]{2,1,0:T(1,128)} %reshape.92), calls=%async_computation | async-start | bytes 8192 | tf_op jit(solution)/shard_map/all_to_all | solution.py:62
  85.3 13.7 %all-to-all-start.1 = ((f32[32,4,8,128]{3,2,1,0:T(8,128)}), f32[32,4,8,128]{3,2,1,0:T(8,128)S(1)}, u32[]{:S(2)}, u32[]{:S(2)}) async-start(f32[32,4,8,128]{3,2,1,0:T(8,128)} %copy.35), calls=%async_computation.1 | async-start | bytes 1048576 | tf_op jit(solution)/shard_map/all_to_all | solution.py:64
where the time goes:
time: 101 us; the launch traced here: 100 us
  blocking collectives  50.6 us (50%)
  matrix products  13.6 us (13%)
  starting transfers between devices  11.8 us (12%)
  waiting for transfers between devices  10.6 us (10%)
  other arithmetic  6.56 us (6%)
  local copies, waits for them, and re-layouts  6.25 us (6%)
    all_gather x1, blocking collectives, on_device(): lax.all_gather(queries, 'seq', axis=0, tiled=True)  14 us
    all_gather x1, blocking collectives, on_device(): lax.all_gather(page_slot, 'seq', axis=0, tiled=True)  13.3 us
    all_gather x1, blocking collectives, on_device(): lax.all_gather(page_owner, 'seq', axis=0, tiled=True)  13.3 us
    unnamed x1, blocking collectives  9.92 us
    all_to_all x1, waiting for transfers between devices, on_device(): lax.all_to_all(request_out, 'seq', split_axis=0, concat_axis=0, tiled=True)  7.67 us
    dot_general x1, matrix products, on_device(): jnp.einsum('pkgd,pktd->pkgt', slot_queries, keys, preferred_element_type=...  6.94 us
    all_to_all x1, starting transfers between devices, on_device(): lax.all_to_all(request_max, 'seq', split_axis=0, concat_axis=0, tiled=True)  5.04 us
    dot_general x1, matrix products, on_device(): jnp.einsum('pkgt,pktd->pkgd', weights.astype(jnp.bfloat16), values, prefe...  4.72 us
  transfers between devices with their start and end apart: 3, of which 2 were waited for; matrix products, arithmetic and copies ran while one was open for 11% of the time, Pallas kernels for 0%

commit v1 on v0

--- a/solution.py
+++ b/solution.py
@@ -5,6 +5,11 @@
 from jax.sharding import PartitionSpec as P
 
 masked_score = -1e30
+
+
+def all_by_exchange(x, axis, along):
+    repeated = jnp.stack([x] * lax.axis_size(axis))
+    return jnp.concatenate(lax.all_to_all(repeated, axis, 0, 0), axis=along)
 
 
 def on_device(queries, page_owner, page_slot, lengths, keys, values):
@@ -18,7 +23,7 @@
     most_pages = page_owner.shape[1]
     page_index = jnp.arange(most_pages, dtype=jnp.int32)
     all_queries, all_owner, all_slot, all_length = (
-        lax.all_gather(queries, "seq", axis=0, tiled=True),
+        all_by_exchange(queries, "seq", 0),
         lax.all_gather(page_owner, "seq", axis=0, tiled=True),
         lax.all_gather(page_slot, "seq", axis=0, tiled=True),
         lax.all_gather(lengths, "seq", axis=0, tiled=True),

time: 101 us -> 94 us (0.931)
  blocking collectives: 50.6 us -> 35.5 us
  starting transfers between devices: 11.8 us -> 18.7 us
  local copies, waits for them, and re-layouts: 6.25 us -> 7.82 us
    all_gather x1 -> x0, blocking collectives: 14 us -> none  [on_device(): lax.all_gather(queries, 'seq', axis=0, tiled=True)]
    all_to_all x0 -> x1, starting transfers between devices: none -> 6.35 us  [all_by_exchange(): return jnp.concatenate(lax.all_to_all(repeated, axis, 0, 0), axis=along)]
    another operation x0 -> x1, local copies, waits for them, and re-layouts: none -> 1.57 us  [all_by_exchange(): repeated = jnp.stack([x] * lax.axis_size(axis))]
    unnamed x1, blocking collectives: 9.92 us -> 8.78 us
  transfers between devices with their start and end apart: 3 -> 4, of which waited for: 2 -> 2; matrix products, arithmetic and copies ran while one was open for 11% -> 17% of each run, Pallas kernels for 0% -> 0%
where the time goes in v1:
time: 94 us; the launch traced here: 93.5 us
  blocking collectives  35.5 us (38%)
  starting transfers between devices  18.7 us (20%)
  matrix products  13.6 us (14%)
  waiting for transfers between devices  10.6 us (11%)
  local copies, waits for them, and re-layouts  7.82 us (8%)
  other arithmetic  6.57 us (7%)
    all_gather x1, blocking collectives, on_device(): lax.all_gather(page_owner, 'seq', axis=0, tiled=True)  13.3 us
    all_gather x1, blocking collectives, on_device(): lax.all_gather(page_slot, 'seq', axis=0, tiled=True)  13.3 us
    unnamed x1, blocking collectives  8.78 us
    all_to_all x1, waiting for transfers between devices, on_device(): lax.all_to_all(request_out, 'seq', split_axis=0, concat_axis=0, tiled=True)  7.71 us
    dot_general x1, matrix products, on_device(): jnp.einsum('pkgd,pktd->pkgt', slot_queries, keys, preferred_element_type=...  6.94 us
    all_to_all x1, starting transfers between devices, all_by_exchange(): return jnp.concatenate(lax.all_to_all(repeated, axis, 0, 0), axis=along)  6.35 us
    all_to_all x1, starting transfers between devices, on_device(): lax.all_to_all(request_max, 'seq', split_axis=0, concat_axis=0, tiled=True)  5.04 us
    dot_general x1, matrix products, on_device(): jnp.einsum('pkgt,pktd->pkgd', weights.astype(jnp.bfloat16), values, prefe...  4.72 us
  transfers between devices with their start and end apart: 4, of which 2 were waited for; matrix products, arithmetic and copies ran while one was open for 17% of the time, Pallas kernels for 0%

profile of v1, /device:TPU:0, one launch (start us, length us, event | category | flops | bytes accessed | tf_op | source)
XLA Modules:
  0.0 93.5 jit_solution(5887006460311330490)
XLA Ops:
  0.0 1.6 %stack.2 = bf16[4,8,32,128]{3,2,1,0:T(8,128)(2,1)} broadcast(bf16[8,32,128]{2,1,0:T(8,128)(2,1)} %param.6), dimensions={1,2,3} | broadcast | bytes 327680 | tf_op jit(solution)/shard_map/stack | solution.py:11
  1.6 6.3 %all-to-all-start = ((bf16[4,8,32,128]{3,2,1,0:T(8,128)(2,1)}), bf16[4,8,32,128]{3,2,1,0:T(8,128)(2,1)S(1)}, u32[]{:S(2)}, u32[]{:S(2)}) async-start(bf16[4,8,32,128]{3,2,1,0:T(8,128)(2,1)} %stack.2), calls=%async_computation | async-start | bytes 524288 | tf_op jit(solution)/shard_map/all_to_all | solution.py:12
  7.9 1.2 %dynamic-slice = u32[1]{0:T(128)} dynamic-slice(u32[32]{0:T(128)} %constant.28, u32[]{:T(128)S(6)} %add), dynamic_slice_sizes={1} | dynamic-slice | bytes 12
  9.8 0.9 dynamic-update-slice
  10.7 8.8 %all-reduce = s32[32]{0:T(128)S(1)} all-reduce(s32[32]{0:T(128)S(1)} %dynamic-update-slice), channel_id=1, replica_groups=mesh['groups'=2,'seq'=4,'head'=2,'rep'=2] {'seq'}, use_global_device_ids=true, to_apply=%add | all-reduce | flops 32 | bytes 256
  19.5 13.3 %all_gather.9 = s32[32,128]{1,0:T(8,128)S(1)} all-gather(s32[8,128]{1,0:T(8,128)} %param.7), channel_id=1, replica_groups=mesh['groups'=2,'seq'=4,'head'=2,'rep'=2] {'seq'}, dimensions={0}, use_global_device_ids=true | all-gather | bytes 20480 | tf_op jit(solution)/shard_map/all_gather | solution.py:27
  32.8 13.3 %all_gather.11 = s32[32,128]{1,0:T(8,128)S(1)} all-gather(s32[8,128]{1,0:T(8,128)} %param.8), channel_id=1, replica_groups=mesh['groups'=2,'seq'=4,'head'=2,'rep'=2] {'seq'}, dimensions={0}, use_global_device_ids=true | all-gather | bytes 20480 | tf_op jit(solution)/shard_map/all_gather | solution.py:28
  46.3 1.2 %fusion.4 = pred[64,32]{1,0:T(8,128)(4,1)S(1)} fusion(s32[32,128]{1,0:T(8,128)S(1)} %all_gather.11, pred[32,128]{1,0:T(8,128)(4,1)S(1)} %compare_and_fusion), kind=kLoop, calls=%fused_computation.10 | loop fusion | flops 784384 | bytes 22528 | tf_op jit(solution)/shard_map/reduce_or | solution.py:37
  47.6 1.2 %select_reduce_fusion = s32[64]{0:T(128)S(1)} fusion(s32[32,128]{1,0:T(8,128)S(1)} %subtract_clamp_fusion, s32[32,128]{1,0:T(8,128)S(1)} %all_gather.11, pred[32,128]{1,0:T(8,128)(4,1)S(1)} %compare_and_fusion), kind=kLoop, calls=%fused_computation.7 | loop fusion | flops 1048512 | bytes 37120 | tf_op jit(solution)/shard_map/reduce_sum | solution.py:38
  48.9 0.3 fusion.1
  49.3 6.9 %fusion.22 = (f32[64,4,8]{2,1,0:T(4,128)S(1)}, f32[64,4,8,128]{3,2,1,0:T(8,128)S(1)}) fusion(bf16[64,4,8,128]{3,2,1,0:T(8,128)(2,1)S(1)} %bitcast.22, bf16[64,4,128,128]{3,2,1,0:T(8,128)(2,1)} %param.10, pred[64,128]{1,0:T(8,128)(4,1)S(1)} %iota_compare_fusion.1), kind=kOutput, calls=%fused_computation.38 | convolution fusion | flops 67893248 | bytes 9977856 | tf_op jit(solution)/shard_map/pkgd,pktd->pkgt/dot_general | solution.py:47
  56.3 0.8 fusion.5
  57.2 0.2 select_reduce_fusion.1
  57.4 0.4 multiply_reduce_fusion
  57.9 0.7 reshape.92
  58.6 3.2 %all-to-all-start.3 = ((f32[4,1,256]{2,1,0:T(1,128)}), f32[4,1,256]{2,1,0:T(1,128)S(1)}, u32[]{:S(2)}, u32[]{:S(2)}) async-start(f32[4,1,256]{2,1,0:T(1,128)} %reshape.92), calls=%async_computation.3 | async-start | bytes 8192 | tf_op jit(solution)/shard_map/all_to_all | solution.py:68
  61.9 4.7 %fusion.7 = f32[64,4,8,128]{3,2,1,0:T(8,128)S(1)} fusion(bf16[64,4,128,128]{3,2,1,0:T(8,128)(2,1)} %param.11, f32[64,4,8,128]{3,2,1,0:T(8,128)S(1)} %get-tuple-element.8, f32[64,4,8]{2,1,0:T(4,128)S(1)} %get-tuple-element.7, pred[64,128]{1,0:T(8,128)(4,1)S(1)} %iota_compare_fusion.1), kind=kOutput, calls=%fused_computation.13 | convolution fusion | flops 67895296 | bytes 10502144 | tf_op jit(solution)/shard_map/pkgt,pktd->pkgd/dot_general | solution.py:56
  66.7 0.7 reshape.90
  67.4 5.0 %all-to-all-start.1 = ((f32[4,1,256]{2,1,0:T(1,128)}), f32[4,1,256]{2,1,0:T(1,128)S(1)}, u32[]{:S(2)}, u32[]{:S(2)}) async-start(f32[4,1,256]{2,1,0:T(1,128)} %reshape.90), calls=%async_computation.1 | async-start | bytes 8192 | tf_op jit(solution)/shard_map/all_to_all | solution.py:67
  72.5 1.6 %convolution_bitcast_fusion = f32[32,4,8,128]{3,0,2,1:T(8,128)S(1)} fusion(f32[64,4,8,128]{3,2,1,0:T(8,128)S(1)} %fusion.7, f32[32,4,8]{0,2,1:T(8,128)S(1)} %select_reduce_fusion.1, f32[64,4,8]{0,2,1:T(8,128)S(1)} %copy.30, pred[32,64]{1,0:T(8,128)(4,1)S(1)} %copy.29), kind=kOutput, calls=%fused_computation.4 | convolution fusion | flops 100859904 | bytes 1587200 | tf_op jit(solution)/shard_map/rpkg,pkgd->rkgd/dot_general | solution.py:65
  74.1 1.1 %copy.35 = f32[32,4,8,128]{3,2,1,0:T(8,128)} copy(f32[32,4,8,128]{3,0,2,1:T(8,128)S(1)} %convolution_bitcast_fusion) | data formatting | bytes 1048576 | tf_op jit(solution)/shard_map/rpkg,pkgd->rkgd/transpose | solution.py:65
  75.2 2.8 %all-to-all-done.1 = f32[4,1,256]{2,1,0:T(1,128)S(1)} async-done(((f32[4,1,256]{2,1,0:T(1,128)}), f32[4,1,256]{2,1,0:T(1,128)S(1)}, u32[]{:S(2)}, u32[]{:S(2)}) %all-to-all-start.1) | async-done | bytes 4128 | tf_op jit(solution)/shard_map/all_to_all | solution.py:67
  78.1 4.1 %all-to-all-start.2 = ((f32[32,4,8,128]{3,2,1,0:T(8,128)}), f32[32,4,8,128]{3,2,1,0:T(8,128)S(1)}, u32[]{:S(2)}, u32[]{:S(2)}) async-start(f32[32,4,8,128]{3,2,1,0:T(8,128)} %copy.35), calls=%async_computation.2 | async-start | bytes 1048576 | tf_op jit(solution)/shard_map/all_to_all | solution.py:69
  82.1 0.5 broadcast.57
  82.6 0.7 reduce
  83.3 0.1 reshape.93
  83.5 0.7 reduce.1
  84.2 0.1 reshape.91
  84.3 0.1 copy.33
  84.7 7.7 %all-to-all-done.2 = f32[32,4,8,128]{3,2,1,0:T(8,128)S(1)} async-done(((f32[32,4,8,128]{3,2,1,0:T(8,128)}), f32[32,4,8,128]{3,2,1,0:T(8,128)S(1)}, u32[]{:S(2)}, u32[]{:S(2)}) %all-to-all-start.2) | async-done | bytes 524320 | tf_op jit(solution)/shard_map/all_to_all | solution.py:69
  92.4 0.3 fusion.9
  92.8 0.7 fusion.19
  (18 shorter events, 1.1 us)
Async XLA Ops:
  1.6 47.3 %all-to-all-start = ((bf16[4,8,32,128]{3,2,1,0:T(8,128)(2,1)}), bf16[4,8,32,128]{3,2,1,0:T(8,128)(2,1)S(1)}, u32[]{:S(2)}, u32[]{:S(2)}) async-start(bf16[4,8,32,128]{3,2,1,0:T(8,128)(2,1)} %stack.2), calls=%async_computation | async-start | bytes 524288 | tf_op jit(solution)/shard_map/all_to_all | solution.py:12
  58.6 8.8 %all-to-all-start.3 = ((f32[4,1,256]{2,1,0:T(1,128)}), f32[4,1,256]{2,1,0:T(1,128)S(1)}, u32[]{:S(2)}, u32[]{:S(2)}) async-start(f32[4,1,256]{2,1,0:T(1,128)} %reshape.92), calls=%async_computation.3 | async-start | bytes 8192 | tf_op jit(solution)/shard_map/all_to_all | solution.py:68
  67.4 10.6 %all-to-all-start.1 = ((f32[4,1,256]{2,1,0:T(1,128)}), f32[4,1,256]{2,1,0:T(1,128)S(1)}, u32[]{:S(2)}, u32[]{:S(2)}) async-start(f32[4,1,256]{2,1,0:T(1,128)} %reshape.90), calls=%async_computation.1 | async-start | bytes 8192 | tf_op jit(solution)/shard_map/all_to_all | solution.py:67
  78.1 14.3 %all-to-all-start.2 = ((f32[32,4,8,128]{3,2,1,0:T(8,128)}), f32[32,4,8,128]{3,2,1,0:T(8,128)S(1)}, u32[]{:S(2)}, u32[]{:S(2)}) async-start(f32[32,4,8,128]{3,2,1,0:T(8,128)} %copy.35), calls=%async_computation.2 | async-start | bytes 1048576 | tf_op jit(solution)/shard_map/all_to_all | solution.py:69
